TPU v7x, 32 devices: a whole 2x2x4 slice. The times are simulated.
32 devices in a mesh: expert: 2 (over core), task: 4 (over y, x), shard: 4 (over z).
Axes of the slice: x: 2, y: 2, z: 4, core: 2. Of those that a mesh axis runs over, the one named last changes fastest.
Arguments:
- weights: bfloat16 [4, 2, 8192, 2048], P('task', None, ('expert', 'shard')), may hold values from -6 to 6
- fisher: bfloat16 [4, 2, 8192, 2048], P('task', None, ('expert', 'shard')), may hold values from 0.049804688 to 5
- base_weights: bfloat16 [2, 8192, 2048], P('expert', 'task', 'shard'), may hold values from -6 to 6
- tile_list: int32 [4, 2, 8, 4], P('task'), may hold values from 0 to 7, as said below
- tile_count: int32 [4, 2, 8], P('task'), may hold values from 0 to 4, as said below
Outputs:
- merged: bfloat16 [2, 8192, 2048], P('expert', 'task', 'shard')
Inputs may be any that keep to these rules, and one draw needn't show every extreme that they name: `tile_list`: for each fine-fit, expert and row block the first tile_count entries are distinct tiles of the block, numbered 0 to 7, in ascending order; the remaining entries are 0. `tile_count`: 4 is reached, and for each fine-fit some expert has 4 in every row block.
All inputs are finite; a program needn't handle non-finite values.
Results may differ from a plain program's by a relative error of at most 0.006.
Values may be sent and summed in bfloat16 or wider, within the bound.
A program may use at most 128 MiB of HBM per device.

v0:
```python
import jax
import jax.numpy as jnp
from jax import lax
from jax.sharding import PartitionSpec as P

TILE = 128


PRIOR_WEIGHT = 0.5


def selection(listed, counts, per_block):
    slot_number = jnp.arange(listed.shape[-1], dtype=jnp.int32)
    slot_live = slot_number[None, :] < counts[:, None]
    matches = (
        listed[:, :, None] == jnp.arange(per_block, dtype=jnp.int32)[None, None, :]
    ) & slot_live[:, :, None]
    return matches.astype(jnp.bfloat16)


def masked_terms(picked, weight_tiles, fisher_tiles):
    kept_tiles = jnp.sum(picked.astype(jnp.float32), axis=1)[:, :, None, None]
    fisher_now = fisher_tiles.astype(jnp.float32) * kept_tiles
    term_full = (fisher_now * weight_tiles.astype(jnp.float32)).astype(jnp.bfloat16)
    share_full = fisher_now.astype(jnp.bfloat16)
    return (term_full, share_full)


def local(weights, fisher, base_weights, tile_list, tile_count):
    experts = weights.shape[1]
    block_rows = weights.shape[2]
    columns = weights.shape[3]
    per_block = block_rows // TILE
    shard_count = lax.axis_size("shard")
    expert_count = lax.axis_size("expert")
    task_count = lax.axis_size("task")
    block_count = expert_count * shard_count
    column_piece = columns // shard_count
    block_index = lax.axis_index("expert") * shard_count + lax.axis_index("shard")
    own_list = lax.dynamic_index_in_dim(tile_list[0], block_index, 1, keepdims=False)
    own_count = lax.dynamic_index_in_dim(tile_count[0], block_index, 1, keepdims=False)
    picked = selection(own_list, own_count, per_block)
    weight_tiles = weights[0].reshape(experts, per_block, TILE, columns)
    fisher_tiles = fisher[0].reshape(experts, per_block, TILE, columns)
    sub_rows = block_rows // task_count
    term_full, share_full = masked_terms(picked, weight_tiles, fisher_tiles)
    term_rows = term_full.reshape(experts, block_rows, columns).astype(jnp.float32)
    share_rows = share_full.reshape(experts, block_rows, columns).astype(jnp.float32)
    summed_term, summed_share = (
        lax.psum_scatter(
            term_rows.astype(jnp.bfloat16), "task", scatter_dimension=1, tiled=True
        ).astype(jnp.float32),
        lax.psum_scatter(
            share_rows.astype(jnp.bfloat16), "task", scatter_dimension=1, tiled=True
        ).astype(jnp.float32),
    )
    sent_term = summed_term.reshape(experts, 1, 1, sub_rows, shard_count, column_piece)
    sent_share = summed_share.reshape(experts, 1, 1, sub_rows, shard_count, column_piece)
    moved_term, moved_share = (
        lax.all_to_all(
            lax.all_to_all(
                sent_term.astype(jnp.bfloat16), "expert", split_axis=0, concat_axis=1, tiled=True
            ),
            "shard",
            split_axis=4,
            concat_axis=2,
            tiled=True,
        ).astype(sent_term.dtype),
        lax.all_to_all(
            lax.all_to_all(
                sent_share.astype(jnp.bfloat16), "expert", split_axis=0, concat_axis=1, tiled=True
            ),
            "shard",
            split_axis=4,
            concat_axis=2,
            tiled=True,
        ).astype(sent_share.dtype),
    )
    group = block_count // task_count
    moved_term = moved_term.reshape(task_count, group, 1, sub_rows, column_piece)
    moved_share = moved_share.reshape(task_count, group, 1, sub_rows, column_piece)
    final_term, final_share = (
        lax.all_to_all(
            moved_term.astype(jnp.bfloat16), "task", split_axis=0, concat_axis=2, tiled=True
        ).astype(moved_term.dtype),
        lax.all_to_all(
            moved_share.astype(jnp.bfloat16), "task", split_axis=0, concat_axis=2, tiled=True
        ).astype(moved_share.dtype),
    )
    numerator = final_term.reshape(1, group * task_count * sub_rows, column_piece)
    denominator = final_share.reshape(1, group * task_count * sub_rows, column_piece)
    merged = (numerator + PRIOR_WEIGHT * base_weights.astype(jnp.float32)) / (
        denominator + PRIOR_WEIGHT
    )
    return merged.astype(jnp.bfloat16)


def solution(mesh):
    in_specs = (
        P("task", None, ("expert", "shard"), None),
        P("task", None, ("expert", "shard"), None),
        P("expert", "task", "shard"),
        P("task", None, None, None),
        P("task", None, None),
    )
    out_specs = P("expert", "task", "shard")
    return jax.shard_map(local, mesh=mesh, in_specs=in_specs, out_specs=out_specs, check_vma=False)
```

profile of v0, /device:TPU:3, one launch (start us, length us, event | category | flops | bytes accessed | tf_op | source)
XLA Modules:
  0.0 401.9 jit_solution(1500051805483809366)
XLA Ops:
  6.5 0.0 copy-start
  6.5 0.0 reduce-scatter.3.cloned.1.call-start
  6.5 0.9 dynamic-slice_reduce_fusion.1
  7.4 0.1 iota_compare_fusion.1
  7.5 0.0 copy-done
  7.5 0.2 dynamic-slice_reduce_fusion
  7.7 0.1 convert_reduce_fusion
  7.8 0.1 broadcast_bitcast_fusion
  7.9 11.9 %copy.25 = bf16[1,2,1024,2048]{2,3,1,0:T(8,128)(2,1)} copy(bf16[1,2,1024,2048]{3,2,1,0:T(8,128)(2,1)} %param.5) | data formatting | bytes 16777216 | tf_op args[0]
  19.8 11.9 %copy.24 = bf16[1,2,1024,2048]{2,3,1,0:T(8,128)(2,1)} copy(bf16[1,2,1024,2048]{3,2,1,0:T(8,128)(2,1)} %param.6) | data formatting | bytes 16777216 | tf_op args[1]
  31.7 12.4 %fusion = (bf16[2,1024,2048]{1,2,0:T(8,128)(2,1)}, bf16[2,1024,2048]{1,2,0:T(8,128)(2,1)}) fusion(bf16[1,2,1024,2048]{2,3,1,0:T(8,128)(2,1)} %copy.25, bf16[1,2,1024,2048]{2,3,1,0:T(8,128)(2,1)} %copy.24, f32[2,1024]{1,0:T(2,128)S(1)} %bitcast.56), kind=kLoop, calls=%fused_computation.1 | loop fusion | flops 25165824 | bytes 33562624 | tf_op jit(solution)/shard_map/convert_element_type | solution.py:24
  44.0 0.0 reduce-scatter.3.cloned.1.call-update
  44.0 0.0 reduce-scatter.5.cloned.1.call-start
  44.1 0.7 reduce-scatter.5.cloned.1.call-update
  44.8 86.8 %reduce-scatter.3.cloned.1.call-done = bf16[2,256,2048]{1,2,0:T(8,128)(2,1)} async-done(((bf16[2,1024,2048]{1,2,0:T(8,128)(2,1)}), bf16[2,256,2048]{1,2,0:T(8,128)(2,1)}) %reduce-scatter.3.cloned.1.call-update) | async-done | bytes 2097168 | tf_op jit(solution)/shard_map/reduce_scatter | solution.py:50
  131.6 4.6 %all-to-all-start = ((bf16[2,1,1,256,4,512]{3,5,4,2,1,0:T(8,128)(2,1)}), bf16[2,1,1,256,4,512]{3,5,4,2,1,0:T(8,128)(2,1)S(1)}, u32[]{:S(2)}, u32[]{:S(2)}) async-start(bf16[2,1,1,256,4,512]{3,5,4,2,1,0:T(8,128)(2,1)} %bitcast.55), calls=%async_computation.1 | async-start | bytes 4194304 | tf_op jit(solution)/shard_map/all_to_all | solution.py:61
  136.2 84.8 %reduce-scatter.5.cloned.1.call-done = bf16[2,256,2048]{1,2,0:T(8,128)(2,1)} async-done(((bf16[2,1024,2048]{1,2,0:T(8,128)(2,1)}), bf16[2,256,2048]{1,2,0:T(8,128)(2,1)}) %reduce-scatter.5.cloned.1.call-update) | async-done | bytes 2097168 | tf_op jit(solution)/shard_map/reduce_scatter | solution.py:53
  221.0 0.0 all-to-all-done
  221.0 5.6 %all-to-all-start.3 = ((bf16[2,1,1,256,4,512]{3,5,4,2,1,0:T(8,128)(2,1)}), bf16[2,1,1,256,4,512]{3,5,4,2,1,0:T(8,128)(2,1)}, u32[]{:S(2)}, u32[]{:S(2)}) async-start(bf16[2,1,1,256,4,512]{3,5,4,2,1,0:T(8,128)(2,1)} %bitcast.54), calls=%async_computation.5 | async-start | bytes 4194304 | tf_op jit(solution)/shard_map/all_to_all | solution.py:70
  226.6 1.4 copy.27
  228.1 1.2 all-to-all-done.3
  229.3 4.3 %all-to-all-start.1 = ((bf16[1,2,1,256,4,512]{3,5,1,2,0,4:T(8,128)(2,1)}), bf16[1,2,1,256,4,512]{3,5,1,2,0,4:T(8,128)(2,1)S(1)}, u32[]{:S(2)}, u32[]{:S(2)}) async-start(bf16[1,2,1,256,4,512]{3,5,1,2,0,4:T(8,128)(2,1)} %copy.27), calls=%async_computation.2 | async-start | bytes 4194304 | tf_op jit(solution)/shard_map/all_to_all | solution.py:60
  233.6 3.0 copy.32
  236.6 44.7 %all-to-all-done.1 = bf16[1,2,1,256,4,512]{3,5,1,2,0,4:T(8,128)(2,1)S(1)} async-done(((bf16[1,2,1,256,4,512]{3,5,1,2,0,4:T(8,128)(2,1)}), bf16[1,2,1,256,4,512]{3,5,1,2,0,4:T(8,128)(2,1)S(1)}, u32[]{:S(2)}, u32[]{:S(2)}) %all-to-all-start.1) | async-done | bytes 2097184 | tf_op jit(solution)/shard_map/all_to_all | solution.py:60
  281.3 4.5 %all-to-all-start.4 = ((bf16[1,2,1,256,4,512]{3,5,1,2,0,4:T(8,128)(2,1)}), bf16[1,2,1,256,4,512]{3,5,1,2,0,4:T(8,128)(2,1)}, u32[]{:S(2)}, u32[]{:S(2)}) async-start(bf16[1,2,1,256,4,512]{3,5,1,2,0,4:T(8,128)(2,1)} %copy.32), calls=%async_computation.6 | async-start | bytes 4194304 | tf_op jit(solution)/shard_map/all_to_all | solution.py:69
  285.8 2.4 copy.28
  288.2 45.4 %all-to-all-done.4 = bf16[1,2,1,256,4,512]{3,5,1,2,0,4:T(8,128)(2,1)} async-done(((bf16[1,2,1,256,4,512]{3,5,1,2,0,4:T(8,128)(2,1)}), bf16[1,2,1,256,4,512]{3,5,1,2,0,4:T(8,128)(2,1)}, u32[]{:S(2)}, u32[]{:S(2)}) %all-to-all-start.4) | async-done | bytes 2097184 | tf_op jit(solution)/shard_map/all_to_all | solution.py:69
  333.6 3.9 all-to-all-start.2
  337.5 4.1 %copy.33 = bf16[1,2,1,256,4,512]{5,3,4,1,2,0:T(8,128)(2,1)} copy(bf16[1,2,1,256,4,512]{3,5,1,2,0,4:T(8,128)(2,1)} %all-to-all-done.4) | data formatting | bytes 4194304 | tf_op jit(solution)/shard_map/all_to_all | solution.py:69
  341.6 19.1 %all-to-all-done.2 = bf16[4,2,1,256,512]{4,3,1,2,0:T(8,128)(2,1)S(1)} async-done(((bf16[4,2,1,256,512]{4,3,1,2,0:T(8,128)(2,1)}), bf16[4,2,1,256,512]{4,3,1,2,0:T(8,128)(2,1)S(1)}, u32[]{:S(2)}, u32[]{:S(2)}) %all-to-all-start.2) | async-done | bytes 2097184 | tf_op jit(solution)/shard_map/all_to_all | solution.py:83
  360.7 5.6 %all-to-all-start.5 = ((bf16[4,2,1,256,512]{4,3,1,2,0:T(8,128)(2,1)}), bf16[4,2,1,256,512]{4,3,1,2,0:T(8,128)(2,1)}, u32[]{:S(2)}, u32[]{:S(2)}) async-start(bf16[4,2,1,256,512]{4,3,1,2,0:T(8,128)(2,1)} %bitcast.53), calls=%async_computation.7 | async-start | bytes 4194304 | tf_op jit(solution)/shard_map/all_to_all | solution.py:86
  366.3 2.5 bitcast_convert_fusion
  368.8 0.0 copy-start.3
  368.8 20.8 %all-to-all-done.5 = bf16[4,2,1,256,512]{4,3,1,2,0:T(8,128)(2,1)} async-done(((bf16[4,2,1,256,512]{4,3,1,2,0:T(8,128)(2,1)}), bf16[4,2,1,256,512]{4,3,1,2,0:T(8,128)(2,1)}, u32[]{:S(2)}, u32[]{:S(2)}) %all-to-all-start.5) | async-done | bytes 2097184 | tf_op jit(solution)/shard_map/all_to_all | solution.py:86
  389.6 0.0 copy-start.2
  389.6 0.0 copy-start.1
  389.6 2.3 convert_add_fusion
  391.9 0.0 copy-done.3
  391.9 0.5 copy-done.2
  392.4 2.7 fusion.2
  395.1 0.0 copy-done.1
  (1 shorter events, 0.0 us)
Async XLA Ops:
  6.5 1.0 copy-start
  6.5 125.0 %reduce-scatter.3.cloned.1.call-start = ((), (), s32[]{:S(2)}) async-start(), calls=%async_computation.8 | async-start | bytes 10485760 | tf_op jit(solution)/shard_map/reduce_scatter | solution.py:50
  44.0 177.0 %reduce-scatter.5.cloned.1.call-start = ((), (), s32[]{:S(2)}) async-start(), calls=%async_computation.9 | async-start | bytes 10485760 | tf_op jit(solution)/shard_map/reduce_scatter | solution.py:53
  131.6 89.4 %all-to-all-start = ((bf16[2,1,1,256,4,512]{3,5,4,2,1,0:T(8,128)(2,1)}), bf16[2,1,1,256,4,512]{3,5,4,2,1,0:T(8,128)(2,1)S(1)}, u32[]{:S(2)}, u32[]{:S(2)}) async-start(bf16[2,1,1,256,4,512]{3,5,4,2,1,0:T(8,128)(2,1)} %bitcast.55), calls=%async_computation.1 | async-start | bytes 4194304 | tf_op jit(solution)/shard_map/all_to_all | solution.py:61
  221.0 8.3 %all-to-all-start.3 = ((bf16[2,1,1,256,4,512]{3,5,4,2,1,0:T(8,128)(2,1)}), bf16[2,1,1,256,4,512]{3,5,4,2,1,0:T(8,128)(2,1)}, u32[]{:S(2)}, u32[]{:S(2)}) async-start(bf16[2,1,1,256,4,512]{3,5,4,2,1,0:T(8,128)(2,1)} %bitcast.54), calls=%async_computation.5 | async-start | bytes 4194304 | tf_op jit(solution)/shard_map/all_to_all | solution.py:70
  229.3 52.1 %all-to-all-start.1 = ((bf16[1,2,1,256,4,512]{3,5,1,2,0,4:T(8,128)(2,1)}), bf16[1,2,1,256,4,512]{3,5,1,2,0,4:T(8,128)(2,1)S(1)}, u32[]{:S(2)}, u32[]{:S(2)}) async-start(bf16[1,2,1,256,4,512]{3,5,1,2,0,4:T(8,128)(2,1)} %copy.27), calls=%async_computation.2 | async-start | bytes 4194304 | tf_op jit(solution)/shard_map/all_to_all | solution.py:60
  281.3 52.3 %all-to-all-start.4 = ((bf16[1,2,1,256,4,512]{3,5,1,2,0,4:T(8,128)(2,1)}), bf16[1,2,1,256,4,512]{3,5,1,2,0,4:T(8,128)(2,1)}, u32[]{:S(2)}, u32[]{:S(2)}) async-start(bf16[1,2,1,256,4,512]{3,5,1,2,0,4:T(8,128)(2,1)} %copy.32), calls=%async_computation.6 | async-start | bytes 4194304 | tf_op jit(solution)/shard_map/all_to_all | solution.py:69
  333.6 27.1 %all-to-all-start.2 = ((bf16[4,2,1,256,512]{4,3,1,2,0:T(8,128)(2,1)}), bf16[4,2,1,256,512]{4,3,1,2,0:T(8,128)(2,1)S(1)}, u32[]{:S(2)}, u32[]{:S(2)}) async-start(bf16[4,2,1,256,512]{4,3,1,2,0:T(8,128)(2,1)} %bitcast.52), calls=%async_computation.3 | async-start | bytes 4194304 | tf_op jit(solution)/shard_map/all_to_all | solution.py:83
  360.7 28.9 %all-to-all-start.5 = ((bf16[4,2,1,256,512]{4,3,1,2,0:T(8,128)(2,1)}), bf16[4,2,1,256,512]{4,3,1,2,0:T(8,128)(2,1)}, u32[]{:S(2)}, u32[]{:S(2)}) async-start(bf16[4,2,1,256,512]{4,3,1,2,0:T(8,128)(2,1)} %bitcast.53), calls=%async_computation.7 | async-start | bytes 4194304 | tf_op jit(solution)/shard_map/all_to_all | solution.py:86
  368.8 23.1 %copy-start.3 = (bf16[1,2048,512]{2,1,0:T(8,128)(2,1)S(1)}, bf16[1,2048,512]{2,1,0:T(8,128)(2,1)}, u32[]{:S(2)}) copy-start(bf16[1,2048,512]{2,1,0:T(8,128)(2,1)} %param.7) | copy-start | bytes 6291460
  389.6 2.8 copy-start.2
  389.6 5.5 %copy-start.1 = (s32[1,2,8,4]{2,3,1,0:T(4,128)S(1)}, s32[1,2,8,4]{2,3,1,0:T(4,128)}, u32[]{:S(2)}) copy-start(s32[1,2,8,4]{2,3,1,0:T(4,128)} %param.8) | copy-start | bytes 772
Sparse Core Ops, SparseCore 0:
  44.2 87.3 reduce-scatter.2
  134.6 86.3 reduce-scatter.4
where the time goes:
time: 406 us; the launch traced here: 402 us
  waiting for transfers between devices  304 us (75%)
  local copies, waits for them, and re-layouts  36.4 us (9%)
  starting transfers between devices  28.5 us (7%)
  other arithmetic  20 us (5%)
  between operations  13.4 us (3%)
    reduce_scatter x1, waiting for transfers between devices, local(): lax.psum_scatter(term_rows.astype(jnp.bfloat16), 'task', scatter_dimensio...  86.8 us
    reduce_scatter x1, waiting for transfers between devices, local(): lax.psum_scatter(share_rows.astype(jnp.bfloat16), 'task', scatter_dimensi...  84.8 us
    all_to_all x1, waiting for transfers between devices, local(): lax.all_to_all(lax.all_to_all(sent_share.astype(jnp.bfloat16), 'expert',...  45.4 us
    all_to_all x1, waiting for transfers between devices, local(): lax.all_to_all(lax.all_to_all(sent_term.astype(jnp.bfloat16), 'expert', s...  44.7 us
    unnamed x12, local copies, waits for them, and re-layouts  24.4 us
    all_to_all x1, waiting for transfers between devices, local(): lax.all_to_all(moved_share.astype(jnp.bfloat16), 'task', split_axis=0, co...  20.8 us
    all_to_all x1, waiting for transfers between devices, local(): lax.all_to_all(moved_term.astype(jnp.bfloat16), 'task', split_axis=0, con...  19.1 us
    convert_element_type x1, other arithmetic, masked_terms(): (fisher_now * weight_tiles.astype(jnp.float32)).astype(jnp.bfloat16)  12.4 us
  transfers between devices with their start and end apart: 8, of which 7 were waited for; matrix products, arithmetic and copies ran while one was open for 3% of the time, Pallas kernels for 0%

commit v1 on v0

v1 whole, which is shorter than its diff:
```python
import functools

import jax
import jax.numpy as jnp
from jax import lax
from jax.experimental import pallas as pl
from jax.experimental.pallas import tpu as pltpu
from jax.sharding import PartitionSpec as P

TILE = 128
PRIOR_WEIGHT = 0.5
MESH = pl.DeviceIdType.MESH


def pack_body(ids, live, weights, fisher, packed):
    expert, slot = pl.program_id(0), pl.program_id(1)
    kept = live[expert * pl.num_programs(1) + slot].astype(jnp.float32)
    pieces, width = packed.shape[1], packed.shape[-1]
    for piece in range(pieces):
        lanes = pl.ds(piece * width, width)
        share = fisher[0, :, lanes].astype(jnp.float32) * kept
        term = share * weights[0, :, lanes].astype(jnp.float32)
        packed[0, piece, 0, 0] = term.astype(jnp.bfloat16)
        packed[0, piece, 1, 0] = share.astype(jnp.bfloat16)


def pack(ids, live, weights, fisher, pieces):
    experts, rows, columns = weights.shape
    cap = ids.shape[0] // experts
    width = columns // pieces
    tile = pl.BlockSpec(
        (1, TILE, columns), lambda e, k, ids, live: (e, ids[e * cap + k], 0)
    )
    return pl.pallas_call(
        pack_body,
        out_shape=jax.ShapeDtypeStruct(
            (experts, pieces, 2, cap, TILE, width), jnp.bfloat16
        ),
        grid_spec=pltpu.PrefetchScalarGridSpec(
            num_scalar_prefetch=2,
            grid=(experts, cap),
            in_specs=[tile, tile],
            out_specs=pl.BlockSpec(
                (1, pieces, 2, 1, TILE, width), lambda e, k, ids, live: (e, 0, 0, k, 0, 0)
            ),
        ),
        name="pack",
    )(ids, live, weights, fisher)


def exchange_body(sizes, packed, received, send_sem, recv_sem, own_sem):
    experts, tasks, shards = sizes
    blocks = experts * shards
    group = blocks // tasks
    expert, task, shard = (lax.axis_index(a) for a in ("expert", "task", "shard"))
    block = expert * shards + shard
    owner = block // group
    place = block % group
    is_own = owner == task
    order = [(de, ds) for ds in range(shards - 1, -1, -1) for de in range(experts)]

    def outgoing(de, ds):
        to_expert = lax.rem(expert + de, experts)
        to_shard = lax.rem(shard + ds, shards)
        return pltpu.make_async_remote_copy(
            src_ref=packed.at[to_expert, to_shard],
            dst_ref=received.at[task, place],
            send_sem=send_sem.at[de, ds],
            recv_sem=recv_sem.at[task, place],
            device_id=(to_expert, owner, to_shard),
            device_id_type=MESH,
        )

    own = pltpu.make_async_copy(
        packed.at[expert, shard], received.at[task, place], own_sem
    )
    for de, ds in order:
        if (de, ds) == (0, 0):
            pl.when(is_own)(own.start)
            pl.when(jnp.logical_not(is_own))(outgoing(de, ds).start)
        else:
            outgoing(de, ds).start()
    for from_task in range(tasks):
        for at in range(group):
            local = jnp.logical_and(is_own, jnp.logical_and(task == from_task, place == at))
            arriving = pltpu.make_async_remote_copy(
                src_ref=packed.at[0, 0],
                dst_ref=received.at[from_task, at],
                send_sem=send_sem.at[0, 0],
                recv_sem=recv_sem.at[from_task, at],
                device_id=(lax.rem(expert + 1, experts), task, shard),
                device_id_type=MESH,
            )
            pl.when(jnp.logical_not(local))(arriving.wait_recv)
    for de, ds in order:
        if (de, ds) == (0, 0):
            pl.when(is_own)(own.wait)
            pl.when(jnp.logical_not(is_own))(outgoing(de, ds).wait_send)
        else:
            outgoing(de, ds).wait_send()


def exchange(packed, sizes):
    experts, tasks, shards = sizes
    group = experts * shards // tasks
    return pl.pallas_call(
        functools.partial(exchange_body, sizes),
        out_shape=jax.ShapeDtypeStruct((tasks, group) + packed.shape[2:], packed.dtype),
        in_specs=[pl.BlockSpec(memory_space=pl.ANY)],
        out_specs=pl.BlockSpec(memory_space=pl.ANY),
        scratch_shapes=[
            pltpu.SemaphoreType.DMA((experts, shards)),
            pltpu.SemaphoreType.DMA((tasks, group)),
            pltpu.SemaphoreType.DMA,
        ],
        compiler_params=pltpu.CompilerParams(has_side_effects=True),
        name="exchange",
    )(packed)


def merge_body(tasks, slots, live, *refs):
    parts, base, merged = refs[:tasks], refs[tasks], refs[tasks + 1]
    at = pl.program_id(0) * pl.num_programs(1) + pl.program_id(1)
    count = pl.num_programs(0) * pl.num_programs(1)
    numerator = PRIOR_WEIGHT * base[...].astype(jnp.float32)
    denominator = jnp.full(base.shape, PRIOR_WEIGHT, jnp.float32)
    for task, part in enumerate(parts):
        kept = live[task * count + at].astype(jnp.float32)
        numerator += part[0, 0, 0, 0].astype(jnp.float32) * kept
        denominator += part[0, 0, 1, 0].astype(jnp.float32) * kept
    merged[...] = (numerator / denominator).astype(jnp.bfloat16)


def merge(slots, live, received, base):
    tasks, group, _, _, _, width = received.shape
    per_block = slots.shape[0] // (tasks * group)

    def part(task):
        return pl.BlockSpec(
            (1, 1, 2, 1, TILE, width),
            lambda g, j, slots, live: (
                task, g, 0, slots[(task * group + g) * per_block + j], 0, 0
            ),
        )

    rows = pl.BlockSpec((TILE, width), lambda g, j, slots, live: (g * per_block + j, 0))
    return pl.pallas_call(
        functools.partial(merge_body, tasks),
        out_shape=jax.ShapeDtypeStruct(base.shape, jnp.bfloat16),
        grid_spec=pltpu.PrefetchScalarGridSpec(
            num_scalar_prefetch=2,
            grid=(group, per_block),
            in_specs=[part(task) for task in range(tasks)] + [rows],
            out_specs=rows,
        ),
        name="merge",
    )(slots, live, *([received] * tasks), base)


def local(weights, fisher, base_weights, tile_list, tile_count):
    experts, tasks, shards = (lax.axis_size(a) for a in ("expert", "task", "shard"))
    expert, task, shard = (lax.axis_index(a) for a in ("expert", "task", "shard"))
    per_block = weights.shape[2] // TILE
    cap = tile_list.shape[-1]
    group = experts * shards // tasks
    block = expert * shards + shard
    slot_number = jnp.arange(cap, dtype=jnp.int32)

    own_list = lax.dynamic_index_in_dim(tile_list[0], block, 1, keepdims=False)
    own_count = lax.dynamic_index_in_dim(tile_count[0], block, 1, keepdims=False)
    own_live = (slot_number[None, :] < own_count[:, None]).astype(jnp.int32)
    packed = pack(own_list.reshape(-1), own_live.reshape(-1), weights[0], fisher[0], shards)

    marked = jnp.where(slot_number < tile_count[..., None], tile_list, per_block)
    plans = lax.all_gather(marked[0], "task")
    plans = lax.dynamic_index_in_dim(plans, expert, 1, keepdims=False)
    plans = lax.dynamic_slice_in_dim(plans, task * group, group, 1)
    hits = plans[..., None] == jnp.arange(per_block, dtype=jnp.int32)
    slots = jnp.sum(hits * slot_number[:, None], axis=2).astype(jnp.int32)
    live = jnp.any(hits, axis=2).astype(jnp.int32)

    received = exchange(packed, (experts, tasks, shards))
    return merge(slots.reshape(-1), live.reshape(-1), received, base_weights[0])[None]


def solution(mesh):
    in_specs = (
        P("task", None, ("expert", "shard"), None),
        P("task", None, ("expert", "shard"), None),
        P("expert", "task", "shard"),
        P("task", None, None, None),
        P("task", None, None),
    )
    out_specs = P("expert", "task", "shard")
    return jax.shard_map(local, mesh=mesh, in_specs=in_specs, out_specs=out_specs, check_vma=False)
```

time: 406 us -> 228 us (0.56); the launches traced: 402 us -> 228 us
  waiting for transfers between devices: 304 us -> 0 us
  Pallas kernels: 0 us -> 217 us
  local copies, waits for them, and re-layouts: 36.4 us -> 4.5 us
  starting transfers between devices: 28.5 us -> 0 us
  other arithmetic: 20 us -> 0.96 us
  between operations: 13.4 us -> 0.02 us
  blocking collectives: 0 us -> 6.16 us
    pallas_call x0 -> x3, Pallas kernels: none -> 217 us  [the longest x1 193 us: exchange(): pl.pallas_call(functools.partial(exchange_body, sizes), out_shape=jax.Sha...]
    reduce_scatter x2 -> x0, waiting for transfers between devices: 172 us -> none  [the longest x1 86.8 us: local(): lax.psum_scatter(term_rows.astype(jnp.bfloat16), 'task', scatter_dimensio...]
    all_to_all x6 -> x0, waiting for transfers between devices: 131 us -> none  [the longest x1 45.4 us: local(): lax.all_to_all(lax.all_to_all(sent_share.astype(jnp.bfloat16), 'expert',...]
    all_to_all x6 -> x0, starting transfers between devices: 28.4 us -> none  [the longest x1 5.63 us: local(): lax.all_to_all(sent_share.astype(jnp.bfloat16), 'expert', split_axis=0, c...]
    unnamed x12 -> x0, local copies, waits for them, and re-layouts: 24.4 us -> none
    convert_element_type x3 -> x2, other arithmetic: 17.5 us -> 0.07 us  [the longest x1 0.07 us: local(): own_live = (slot_number[None, :] < own_count[:, None]).astype(jnp.int32)]
    all_to_all x4 -> x0, local copies, waits for them, and re-layouts: 11 us -> none  [the longest x1 4.13 us: local(): lax.all_to_all(lax.all_to_all(sent_share.astype(jnp.bfloat16), 'expert',...]
    all_gather x0 -> x1, blocking collectives: none -> 6.16 us  [local(): plans = lax.all_gather(marked[0], 'task')]
  transfers between devices with their start and end apart: 8 -> 0, of which waited for: 7 -> 0; matrix products, arithmetic and copies ran while one was open for 3% -> 0% of each run, Pallas kernels for 0% -> 0%
where the time goes in v1:
time: 228 us
  Pallas kernels  217 us (95%)
  blocking collectives  6.16 us (3%)
  local copies, waits for them, and re-layouts  4.5 us (2%)
    pallas_call x1, Pallas kernels, exchange(): pl.pallas_call(functools.partial(exchange_body, sizes), out_shape=jax.Sha...  193 us
    pallas_call x1, Pallas kernels, merge(): pl.pallas_call(functools.partial(merge_body, tasks), out_shape=jax.ShapeD...  14 us
    pallas_call x1, Pallas kernels, pack(): pl.pallas_call(pack_body, out_shape=jax.ShapeDtypeStruct((experts, pieces...  10 us
    all_gather x1, blocking collectives, local(): plans = lax.all_gather(marked[0], 'task')  6.16 us

profile of v1, /device:TPU:3, one launch (start us, length us, event | category | flops | bytes accessed | tf_op | source)
XLA Modules:
  0.0 228.3 jit_solution(3810448163241272843)
XLA Ops:
  0.0 0.9 dynamic-slice_reduce_fusion.1
  0.9 0.9 dynamic-slice_reduce_fusion
  1.8 0.6 reshape.36.ids
  2.4 0.1 compare_convert_fusion
  2.4 0.7 reshape.38.live
  3.1 0.7 fusion.1
  3.8 6.2 %all_gather.3 = s32[4,2,8,4]{2,3,1,0:T(4,128)S(1)} all-gather(s32[1,2,8,4]{2,3,1,0:T(4,128)S(1)} %fusion.1), channel_id=1, replica_groups=mesh['expert'=2,'task'=4,'shard'=4] {'task'}, dimensions={0}, use_global_device_ids=true | all-gather | bytes 1280 | tf_op jit(solution)/shard_map/all_gather | solution.py:175
  10.0 0.1 constant_dynamic-slice_fusion
  10.0 0.1 copy.9
  10.2 0.1 fusion
  10.2 0.1 select_reduce_fusion
  10.3 0.6 reshape.35.slots
  10.9 0.7 reshape.37.live
  11.6 10.0 %pack.1.packed = bf16[2,4,2,4,128,512]{5,4,3,2,1,0:T(8,128)(2,1)} custom-call(s32[8]{0:T(128)} %reshape.36.ids, s32[8]{0:T(128)} %reshape.38.live, bf16[2,1024,2048]{2,1,0:T(8,128)(2,1)} %bitcast.6, bf16[2,1024,2048]{2,1,0:T(8,128)(2,1)} %bitcast.7), custom_call_target="tpu_custom_call" | custom-call | tf_op jit(solution)/shard_map/pack/pallas_call | solution.py:34
  21.6 192.7 %exchange.1.refs_0_.refs_1_.refs_2_.refs_3_ = bf16[4,2,2,4,128,512]{5,4,3,2,1,0:T(8,128)(2,1)} custom-call(bf16[2,4,2,4,128,512]{5,4,3,2,1,0:T(8,128)(2,1)} %pack.1.packed), custom_call_target="tpu_custom_call" | custom-call | tf_op jit(solution)/shard_map/exchange/pallas_call | solution.py:106
  214.3 14.0 %merge.1 = bf16[2048,512]{1,0:T(8,128)(2,1)} custom-call(s32[64]{0:T(128)} %reshape.35.slots, s32[64]{0:T(128)} %reshape.37.live, bf16[4,2,2,4,128,512]{5,4,3,2,1,0:T(8,128)(2,1)} %exchange.1.refs_0_.refs_1_.refs_2_.refs_3_, bf16[4,2,2,4,128,512]{5,4,3,2,1,0:T(8,128)(2,1)} %exchange.1.refs_0_.refs_1_.refs_2_.refs_3_, ...), custom_call_target="tpu_custom_call" | custom-call | tf_op jit(solution)/shard_map/merge/pallas_call | solution.py:147
  (1 shorter events, 0.0 us)

commit v2 on v1

--- a/solution.py
+++ b/solution.py
@@ -9,6 +9,7 @@
 
 TILE = 128
 PRIOR_WEIGHT = 0.5
+DIRECT = 32
 MESH = pl.DeviceIdType.MESH
 
 
@@ -157,6 +158,286 @@
     )(slots, live, *([received] * tasks), base)
 
 
+def arrive(like, target, send_sem, recv_sem, peer):
+    return pltpu.make_async_remote_copy(
+        src_ref=like, dst_ref=target, send_sem=send_sem, recv_sem=recv_sem,
+        device_id=peer, device_id_type=MESH,
+    )
+
+
+def spread_body(packed, plan, direct, gathered, plans, p_send, p_recv, d_send, d_recv, g_send, g_recv, own_sem):
+    expert, task, shard = (lax.axis_index(a) for a in ("expert", "task", "shard"))
+    block = expert * 4 + shard
+    owner, place = block // 2, block % 2
+    half, x, y = shard // 2, task % 2, task // 2
+    peer = (1 - expert, task, shard)
+    part = (DIRECT, (TILE - DIRECT) // 2)
+    far = pl.ds(pl.multiple_of(2 * (1 - half), 2), 2)
+
+    def straight(de, ds):
+        to_expert, to_shard = (expert + de) % 2, (shard + ds) % 4
+        rows = packed.at[to_expert, to_shard, :, :, pl.ds(0, DIRECT)]
+        return rows, pltpu.make_async_remote_copy(
+            src_ref=rows, dst_ref=direct.at[task, place],
+            send_sem=d_send.at[de, ds], recv_sem=d_recv.at[task, place],
+            device_id=(to_expert, owner, to_shard), device_id_type=MESH,
+        )
+
+    def partial(de, dx):
+        to_expert, to_x = (expert + de) % 2, (x + dx) % 2
+        start = pl.multiple_of(part[0] + part[1] * to_x, 16)
+        rows = packed.at[to_expert, far, :, :, pl.ds(start, part[1])]
+        return rows, pltpu.make_async_remote_copy(
+            src_ref=rows, dst_ref=gathered.at[task],
+            send_sem=g_send.at[de, dx], recv_sem=g_recv.at[task],
+            device_id=(to_expert, 2 * expert + to_x, shard), device_id_type=MESH,
+        )
+
+    def tell(step):
+        return pltpu.make_async_remote_copy(
+            src_ref=plan, dst_ref=plans.at[task],
+            send_sem=p_send.at[step], recv_sem=p_recv.at[task],
+            device_id=(expert, (task + step) % 4, shard), device_id_type=MESH,
+        )
+
+    told = pltpu.make_async_copy(plan, plans.at[task], own_sem.at[2])
+    told.start()
+    for step in range(1, 4):
+        tell(step).start()
+    copies = []
+    for de in range(2):
+        for dx in (1, 0):
+            own = y == expert if (de, dx) == (0, 0) else None
+            copies.append((partial(de, dx), own, gathered.at[task], own_sem.at[0]))
+    for ds in (2, 1, 3, 0):
+        for de in range(2):
+            own = owner == task if (de, ds) == (0, 0) else None
+            copies.append((straight(de, ds), own, direct.at[task, place], own_sem.at[1]))
+    for (rows, copy), own, target, sem in copies:
+        if own is None:
+            copy.start()
+        else:
+            pl.when(own)(pltpu.make_async_copy(rows, target, sem).start)
+            pl.when(jnp.logical_not(own))(copy.start)
+    for source in range(4):
+        come = arrive(plans.at[source], plans.at[source], p_send.at[0], p_recv.at[source], peer)
+        pl.when(task != source)(come.wait_recv)
+        local = jnp.logical_and(y == expert, task == source)
+        come = arrive(gathered.at[source], gathered.at[source], g_send.at[0, 0], g_recv.at[source], peer)
+        pl.when(jnp.logical_not(local))(come.wait_recv)
+        for at in range(2):
+            local = jnp.logical_and(owner == task, jnp.logical_and(task == source, place == at))
+            come = arrive(direct.at[source, at], direct.at[source, at], d_send.at[0, 0], d_recv.at[source, at], peer)
+            pl.when(jnp.logical_not(local))(come.wait_recv)
+    told.wait()
+    for step in range(1, 4):
+        tell(step).wait_send()
+    for (rows, copy), own, target, sem in copies:
+        if own is None:
+            copy.wait_send()
+        else:
+            pl.when(own)(pltpu.make_async_copy(rows, target, sem).wait)
+            pl.when(jnp.logical_not(own))(copy.wait_send)
+
+
+def spread(packed, plan):
+    _, _, _, cap, _, width = packed.shape
+    return pl.pallas_call(
+        spread_body,
+        out_shape=(
+            jax.ShapeDtypeStruct((4, 2, 2, cap, DIRECT, width), packed.dtype),
+            jax.ShapeDtypeStruct((4, 2, 2, cap, (TILE - DIRECT) // 2, width), packed.dtype),
+            jax.ShapeDtypeStruct((4,) + plan.shape, plan.dtype),
+        ),
+        in_specs=[pl.BlockSpec(memory_space=pl.ANY)] * 2,
+        out_specs=(pl.BlockSpec(memory_space=pl.ANY),) * 3,
+        scratch_shapes=[
+            pltpu.SemaphoreType.DMA((4,)),
+            pltpu.SemaphoreType.DMA((4,)),
+            pltpu.SemaphoreType.DMA((2, 4)),
+            pltpu.SemaphoreType.DMA((4, 2)),
+            pltpu.SemaphoreType.DMA((2, 2)),
+            pltpu.SemaphoreType.DMA((4,)),
+            pltpu.SemaphoreType.DMA((3,)),
+        ],
+        compiler_params=pltpu.CompilerParams(has_side_effects=True),
+        name="spread",
+    )(packed, plan)
+
+
+def deliver_body(packed, sums, near, far, n_send, n_recv, f_send, f_recv, own_sem):
+    expert, task, shard = (lax.axis_index(a) for a in ("expert", "task", "shard"))
+    block = expert * 4 + shard
+    owner, place = block // 2, block % 2
+    half, x, y = shard // 2, task % 2, task // 2
+    peer = (1 - expert, task, shard)
+    rest = pl.ds(DIRECT, TILE - DIRECT)
+    is_near = x == half
+
+    def reduced(i):
+        return pltpu.make_async_remote_copy(
+            src_ref=sums.at[i], dst_ref=far.at[shard % 2, x],
+            send_sem=f_send.at[i], recv_sem=f_recv.at[shard % 2, x],
+            device_id=(expert, 2 * y + half, 2 * (1 - half) + i), device_id_type=MESH,
+        )
+
+    def straight(de, di):
+        to_expert = (expert + de) % 2
+        to_shard = 2 * half + (shard + di) % 2
+        rows = packed.at[to_expert, to_shard, :, :, rest]
+        return rows, pltpu.make_async_remote_copy(
+            src_ref=rows, dst_ref=near.at[task, place],
+            send_sem=n_send.at[de, di], recv_sem=n_recv.at[task, place],
+            device_id=(to_expert, owner, to_shard), device_id_type=MESH,
+        )
+
+    for i in range(2):
+        reduced(i).start()
+    own = owner == task
+    for de, di in ((0, 1), (1, 1), (1, 0)):
+        straight(de, di)[1].start()
+    rows, copy = straight(0, 0)
+    kept = pltpu.make_async_copy(rows, near.at[task, place], own_sem)
+    pl.when(own)(kept.start)
+    pl.when(jnp.logical_not(own))(copy.start)
+
+    for at in range(2):
+        for source in range(2):
+            come = arrive(far.at[at, source], far.at[at, source], f_send.at[0], f_recv.at[at, source], peer)
+            pl.when(jnp.logical_not(is_near))(come.wait_recv)
+        for source in range(4):
+            local = jnp.logical_and(own, jnp.logical_and(task == source, place == at))
+            come = arrive(near.at[source, at], near.at[source, at], n_send.at[0, 0], n_recv.at[source, at], peer)
+            pl.when(jnp.logical_and(is_near, jnp.logical_not(local)))(come.wait_recv)
+    for i in range(2):
+        reduced(i).wait_send()
+    for de, di in ((0, 1), (1, 1), (1, 0)):
+        straight(de, di)[1].wait_send()
+    pl.when(own)(kept.wait)
+    pl.when(jnp.logical_not(own))(copy.wait_send)
+
+
+def deliver(packed, sums):
+    _, _, _, cap, _, width = packed.shape
+    return pl.pallas_call(
+        deliver_body,
+        out_shape=(
+            jax.ShapeDtypeStruct((4, 2, 2, cap, TILE - DIRECT, width), packed.dtype),
+            jax.ShapeDtypeStruct((2, 2) + sums.shape[1:], packed.dtype),
+        ),
+        in_specs=[pl.BlockSpec(memory_space=pl.ANY)] * 2,
+        out_specs=(pl.BlockSpec(memory_space=pl.ANY),) * 2,
+        scratch_shapes=[
+            pltpu.SemaphoreType.DMA((2, 2)),
+            pltpu.SemaphoreType.DMA((4, 2)),
+            pltpu.SemaphoreType.DMA((2,)),
+            pltpu.SemaphoreType.DMA((2, 2)),
+            pltpu.SemaphoreType.DMA,
+        ],
+        compiler_params=pltpu.CompilerParams(has_side_effects=True),
+        name="deliver",
+    )(packed, sums)
+
+
+def reduce_body(slots, live, *refs):
+    parts, sums = refs[:4], refs[4]
+    tile = pl.program_id(0)
+    total = jnp.zeros(sums.shape[:2] + sums.shape[3:], jnp.float32)
+    for task, part in enumerate(parts):
+        kept = live[task * pl.num_programs(0) + tile].astype(jnp.float32)
+        total += part[0, :, :, 0].astype(jnp.float32) * kept
+    sums[:, :, 0] = total.astype(jnp.bfloat16)
+
+
+def reduce(slots, live, gathered):
+    rows, width = gathered.shape[-2:]
+    per_block = slots.shape[0] // 4
+
+    def part(task):
+        return pl.BlockSpec(
+            (1, 2, 2, 1, rows, width),
+            lambda j, slots, live: (task, 0, 0, slots[task * per_block + j], 0, 0),
+        )
+
+    return pl.pallas_call(
+        reduce_body,
+        out_shape=jax.ShapeDtypeStruct((2, 2, per_block, rows, width), jnp.bfloat16),
+        grid_spec=pltpu.PrefetchScalarGridSpec(
+            num_scalar_prefetch=2,
+            grid=(per_block,),
+            in_specs=[part(task) for task in range(4)],
+            out_specs=pl.BlockSpec((2, 2, 1, rows, width), lambda j, slots, live: (0, 0, j, 0, 0)),
+        ),
+        name="reduce",
+    )(slots, live, *([gathered] * 4))
+
+
+def finish_body(slots, live, near_flag, *refs):
+    direct, near, far, base, merged = refs[:4], refs[4:8], refs[8], refs[9], refs[10]
+    at = pl.program_id(0) * pl.num_programs(1) + pl.program_id(1)
+    count = pl.num_programs(0) * pl.num_programs(1)
+    kept = [live[task * count + at].astype(jnp.float32) for task in range(4)]
+
+    def settle(rows, numerator, denominator):
+        numerator += PRIOR_WEIGHT * base[rows].astype(jnp.float32)
+        merged[rows] = (numerator / (denominator + PRIOR_WEIGHT)).astype(jnp.bfloat16)
+
+    def added(parts, which):
+        return sum(p[0, 0, which, 0].astype(jnp.float32) * k for p, k in zip(parts, kept))
+
+    settle(pl.ds(0, DIRECT), added(direct, 0), added(direct, 1))
+
+    @pl.when(near_flag[0] == 1)
+    def _():
+        settle(pl.ds(DIRECT, TILE - DIRECT), added(near, 0), added(near, 1))
+
+    @pl.when(near_flag[0] == 0)
+    def _():
+        size = (TILE - DIRECT) // 2
+        for x in range(2):
+            settle(
+                pl.ds(DIRECT + size * x, size),
+                far[0, x, 0, 0].astype(jnp.float32),
+                far[0, x, 1, 0].astype(jnp.float32),
+            )
+
+
+def finish(slots, live, near_flag, direct, near, far, base):
+    width = base.shape[-1]
+    per_block = slots.shape[0] // 8
+
+    def direct_part(task):
+        return pl.BlockSpec(
+            (1, 1, 2, 1, DIRECT, width),
+            lambda g, j, slots, live, flag: (task, g, 0, slots[(task * 2 + g) * per_block + j], 0, 0),
+        )
+
+    def near_part(task):
+        return pl.BlockSpec(
+            (1, 1, 2, 1, TILE - DIRECT, width),
+            lambda g, j, slots, live, flag: (
+                task, g * flag[0], 0, slots[(task * 2 + g) * per_block + j] * flag[0], 0, 0
+            ),
+        )
+
+    far_part = pl.BlockSpec(
+        (1, 2, 2, 1, (TILE - DIRECT) // 2, width),
+        lambda g, j, slots, live, flag: (g * (1 - flag[0]), 0, 0, j * (1 - flag[0]), 0, 0),
+    )
+    rows = pl.BlockSpec((TILE, width), lambda g, j, slots, live, flag: (g * per_block + j, 0))
+    return pl.pallas_call(
+        finish_body,
+        out_shape=jax.ShapeDtypeStruct(base.shape, jnp.bfloat16),
+        grid_spec=pltpu.PrefetchScalarGridSpec(
+            num_scalar_prefetch=3,
+            grid=(2, per_block),
+            in_specs=[direct_part(t) for t in range(4)] + [near_part(t) for t in range(4)] + [far_part, rows],
+            out_specs=rows,
+        ),
+        name="finish",
+    )(slots, live, near_flag, *([direct] * 4), *([near] * 4), far, base)
+
+
 def local(weights, fisher, base_weights, tile_list, tile_count):
     experts, tasks, shards = (lax.axis_size(a) for a in ("expert", "task", "shard"))
     expert, task, shard = (lax.axis_index(a) for a in ("expert", "task", "shard"))
@@ -172,15 +453,30 @@
     packed = pack(own_list.reshape(-1), own_live.reshape(-1), weights[0], fisher[0], shards)
 
     marked = jnp.where(slot_number < tile_count[..., None], tile_list, per_block)
-    plans = lax.all_gather(marked[0], "task")
-    plans = lax.dynamic_index_in_dim(plans, expert, 1, keepdims=False)
-    plans = lax.dynamic_slice_in_dim(plans, task * group, group, 1)
-    hits = plans[..., None] == jnp.arange(per_block, dtype=jnp.int32)
-    slots = jnp.sum(hits * slot_number[:, None], axis=2).astype(jnp.int32)
-    live = jnp.any(hits, axis=2).astype(jnp.int32)
-
+    mine = lax.dynamic_index_in_dim(marked[0], expert, 0, keepdims=False)
+    small = (experts, tasks, shards) == (2, 4, 4)
+    if small:
+        plan = jnp.pad(mine, ((0, 0), (0, 128 - cap)))
+        direct, gathered, plans = spread(packed, plan)
+        plans = plans[:, :, :cap]
+    else:
+        plans = lax.all_gather(marked[0], "task")
+        plans = lax.dynamic_index_in_dim(plans, expert, 1, keepdims=False)
+
+    def lookup(start, count):
+        part = lax.dynamic_slice_in_dim(plans, start, count, 1)
+        hits = part[..., None] == jnp.arange(per_block, dtype=jnp.int32)
+        slots = jnp.sum(hits * slot_number[:, None], axis=2).astype(jnp.int32)
+        return slots.reshape(-1), jnp.any(hits, axis=2).astype(jnp.int32).reshape(-1)
+
+    slots, live = lookup(task * group, group)
+    if small:
+        sums = reduce(*lookup((task // 2) * shards + shard, 1), gathered)
+        near, far = deliver(packed, sums)
+        flag = (task % 2 == shard // 2).astype(jnp.int32).reshape(1)
+        return finish(slots, live, flag, direct, near, far, base_weights[0])[None]
     received = exchange(packed, (experts, tasks, shards))
-    return merge(slots.reshape(-1), live.reshape(-1), received, base_weights[0])[None]
+    return merge(slots, live, received, base_weights[0])[None]
 
 
 def solution(mesh):

time: 228 us -> 183 us (0.80)
  the two profiles are of different devices: /device:TPU:3 before, /device:TPU:1 now
where the time goes in v2:
time: 183 us; the launch traced here: 182 us
  Pallas kernels  175 us (96%)
  local copies, waits for them, and re-layouts  6.87 us (4%)
    pallas_call x1, Pallas kernels, deliver(): pl.pallas_call(deliver_body, out_shape=(jax.ShapeDtypeStruct((4, 2, 2, ca...  76.1 us
    pallas_call x1, Pallas kernels, spread(): pl.pallas_call(spread_body, out_shape=(jax.ShapeDtypeStruct((4, 2, 2, cap...  66.3 us
    pallas_call x1, Pallas kernels, finish(): pl.pallas_call(finish_body, out_shape=jax.ShapeDtypeStruct(base.shape, jn...  14.6 us
    pallas_call x1, Pallas kernels, pack(): pl.pallas_call(pack_body, out_shape=jax.ShapeDtypeStruct((experts, pieces...  10.1 us
    pallas_call x1, Pallas kernels, reduce(): pl.pallas_call(reduce_body, out_shape=jax.ShapeDtypeStruct((2, 2, per_blo...  7.41 us

profile of v2, /device:TPU:1, one launch (start us, length us, event | category | flops | bytes accessed | tf_op | source)
XLA Modules:
  0.0 181.9 jit_solution(935059374586408717)
XLA Ops:
  0.0 0.0 copy-start
  0.0 0.9 dynamic-slice_reduce_fusion
  0.9 0.6 reshape.72.ids
  1.5 0.0 copy-done
  1.5 0.2 fusion.3
  1.7 0.1 compare_convert_fusion
  1.8 0.6 reshape.77.live
  2.3 0.0 copy-start.1
  2.3 10.1 %pack.1.packed = bf16[2,4,2,4,128,512]{5,4,3,2,1,0:T(8,128)(2,1)} custom-call(s32[8]{0:T(128)} %reshape.72.ids, s32[8]{0:T(128)} %reshape.77.live, bf16[2,1024,2048]{2,1,0:T(8,128)(2,1)} %bitcast.11, bf16[2,1024,2048]{2,1,0:T(8,128)(2,1)} %bitcast.12), custom_call_target="tpu_custom_call" | custom-call | tf_op jit(solution)/shard_map/pack/pallas_call | solution.py:35
  12.5 0.0 copy-done.1
  12.5 0.1 copy.8
  12.6 0.6 pad.4.plan
  13.2 66.3 %spread.1 = (bf16[4,2,2,4,32,512]{5,4,3,2,1,0:T(8,128)(2,1)}, bf16[4,2,2,4,48,512]{5,4,3,2,1,0:T(8,128)(2,1)}, s32[4,8,128]{2,1,0:T(8,128)}) custom-call(bf16[2,4,2,4,128,512]{5,4,3,2,1,0:T(8,128)(2,1)} %pack.1.packed, s32[8,128]{1,0:T(8,128)} %pad.4.plan), custom_call_target="tpu_custom_call" | custom-call | tf_op jit(solution)/shard_map/spread/pallas_call | solution.py:245
  79.5 0.7 constant_dynamic-slice_fusion.2
  80.2 0.1 select_reduce_fusion
  80.3 0.6 reshape.73.slots
  80.9 0.1 fusion
  81.0 0.6 reshape.78.live
  81.6 0.7 constant_dynamic-slice_fusion
  82.3 0.1 select_reduce_fusion.1
  82.4 0.6 reshape.76.slots
  83.1 0.1 fusion.1
  83.2 0.7 reshape.81.live
  83.8 7.4 %reduce.7.sums = bf16[2,2,8,48,512]{4,3,2,1,0:T(8,128)(2,1)} custom-call(s32[32]{0:T(128)} %reshape.76.slots, s32[32]{0:T(128)} %reshape.81.live, bf16[4,2,2,4,48,512]{5,4,3,2,1,0:T(8,128)(2,1)} %get-tuple-element.12.refs_0_.refs_1_.refs_2_.refs_3_, bf16[4,2,2,4,48,512]{5,4,3,2,1,0:T(8,128)(2,1)} %get-tuple-element.12.refs_0_.refs_1_.refs_2_.refs_3_, ...), custom_call_target="tpu_custom_call" | custom-call | tf_op jit(solution)/shard_map/reduce/pallas_call | solution.py:362
  91.2 76.1 %deliver.1 = (bf16[4,2,2,4,96,512]{5,4,3,2,1,0:T(8,128)(2,1)}, bf16[2,2,2,8,48,512]{5,4,3,2,1,0:T(8,128)(2,1)}) custom-call(bf16[2,4,2,4,128,512]{5,4,3,2,1,0:T(8,128)(2,1)} %pack.1.packed, bf16[2,2,8,48,512]{4,3,2,1,0:T(8,128)(2,1)} %reduce.7.sums), custom_call_target="tpu_custom_call" | custom-call | tf_op jit(solution)/shard_map/deliver/pallas_call | solution.py:322
  167.4 14.6 %finish.1 = bf16[2048,512]{1,0:T(8,128)(2,1)} custom-call(s32[64]{0:T(128)} %reshape.73.slots, s32[64]{0:T(128)} %reshape.78.live, s32[1]{0:T(128)} %bitcast.4.near_flag, bf16[4,2,2,4,32,512]{5,4,3,2,1,0:T(8,128)(2,1)} %get-tuple-element.11.refs_0_.refs_1_.refs_2_.refs_3_, bf16[4,2,2,4,32,512]{5,4,3,2,1,0:T(8,128)(2,1)} %get-tuple-element.11.refs_0_.refs_1_.refs_2_.refs_3_, ...), custom_call_target="tpu_custom_call" | custom-call | tf_op jit(solution)/shard_map/finish/pallas_call | solution.py:428
  (4 shorter events, 0.0 us)
Async XLA Ops:
  0.0 1.5 copy-start
  2.3 10.1 %copy-start.1 = (s32[1,2,8,4]{2,3,1,0:T(4,128)S(1)}, s32[1,2,8,4]{2,3,1,0:T(4,128)}, u32[]{:S(2)}) copy-start(s32[1,2,8,4]{2,3,1,0:T(4,128)} %param.8) | copy-start | bytes 772
